TPU v7x, 32 devices: a whole 2x2x4 slice. The times are simulated.
32 devices in a mesh: batch: 8 (over z, y), rows: 4 (over x, core).
Axes of the slice: x: 2, y: 2, z: 4, core: 2. Of those that a mesh axis runs over, the one named last changes fastest.
Arguments:
- features: bfloat16 [192, 14, 14, 1024], P(('batch', 'rows')), may hold values from -12 to 12
- grads: bfloat16 [192, 14, 14, 256], P(('batch', 'rows')), may hold values from -12 to 12
- kernel: bfloat16 [3, 3, 256, 1024], replicated, may hold values from -0.125 to 0.125
- vectors: float32 [16, 64, 64], replicated, may hold values from -1 to 1, as said below
- values: float32 [16, 64], replicated, may hold values from 0.05 to 2
Outputs:
- input_grad: bfloat16 [192, 14, 14, 1024], P(('batch', 'rows'))
- kernel_grad: float32 [1024, 3, 3, 256], P(('batch', 'rows'))
Inputs may be any that keep to these rules, and one draw needn't show every extreme that they name: `vectors`: each group's matrix is orthogonal.
All inputs are finite; a program needn't handle non-finite values.
Results may differ from a plain program's by a relative error of at most 0.015.
Values sent between devices are 32-bit elements; how exact they have to be, the bound alone decides.
A program may use at most 128 MiB of HBM per device.

v0:
```python
import functools
import jax
import jax.numpy as jnp
from jax import lax
from jax.experimental import pallas as pl
from jax.experimental.pallas import tpu as pltpu
from jax.sharding import PartitionSpec as P

highest = lax.Precision.HIGHEST
F32, BF16 = jnp.float32, jnp.bfloat16
LANES = 128
VMEM_LIMIT = 63 * 1024 * 1024


def round_up(n, m):
    return (n + m - 1) // m * m


def bit_orders(bits):
    rest = list(range(1, bits))
    first = [0] + rest
    second = [0] + rest[1:2] + rest[:1] + rest[2:]
    third = [0] + rest[2:3] + rest[:2] + rest[3:]
    return [first, second, third]


def slot_of(index, order):
    slot = 0
    count = len(order)
    for step, bit in enumerate(order):
        slot = slot + (index // 2**bit) % 2 * 2 ** (count - 1 - step)
    return slot


def step_kernel(
    sizes, f_ref, g_ref, k_hbm, v_ref, sv_ref, o_ref, share_ref,
    fp, ft, cols, gpad, k_ref, back, w_ref, s_ref, flat, small, total, column, pieces,
    k_sem, send_sem, recv_sem, *scratch
):
    (nb, nr, images, height, width, wide, channels, outputs, per, orders, streams, pixel_total) = sizes
    rows = images * height * wide
    kp = fp.shape[0]
    blocks = channels // LANES
    taps = 3 * outputs
    part_width = 3 * taps // streams
    bits = len(orders[0])
    count = 2**bits
    rp = small.shape[1]
    half = LANES // 2
    base = channels // 2
    image_rows = height * wide
    batch = lax.axis_index("batch")
    row = lax.axis_index("rows")
    index = batch * nr + row

    def bit_of(bit):
        return (index // 2**bit) % 2

    def partner(bit):
        sign = 1 - 2 * bit_of(bit)
        if 2**bit < nr:
            return (batch, row + sign * 2**bit)
        return (batch + sign * (2**bit // nr), row)

    barrier = pltpu.get_barrier_semaphore()
    for bit in range(bits):
        pl.semaphore_signal(
            barrier, inc=1, device_id=partner(bit), device_id_type=pl.DeviceIdType.MESH
        )
    k_copy = pltpu.make_async_copy(k_hbm, k_ref, k_sem)
    k_copy.start()

    fp[pl.ds(rows, kp - rows), :] = jnp.zeros((kp - rows, channels), BF16)
    cols[pl.ds(rows, kp - rows), :] = jnp.zeros((kp - rows, 3 * taps), BF16)
    gpad[...] = jnp.zeros(gpad.shape, F32)

    @pl.loop(0, images)
    def _(b):
        gpad[pl.ds(1, height), pl.ds(1, width), :] = g_ref[b].astype(F32)
        for h in range(height):
            at = pl.multiple_of((b * height + h) * wide, 16)
            fp[pl.ds(at, wide), :] = jnp.zeros((wide, channels), BF16)
            fp[pl.ds(at, width), :] = f_ref[b, h]
        at = pl.multiple_of(b * image_rows, 16)
        for c in range(3):
            shifted = gpad[:, 2 - c : 2 - c + wide, :].astype(BF16)
            for a in range(3):
                first = a * taps + c * outputs
                cols[pl.ds(at, image_rows), first : first + outputs] = shifted[
                    2 - a : 2 - a + height
                ].reshape(image_rows, outputs)

    @pl.loop(0, blocks)
    def _(k):
        at = pl.ds(pl.multiple_of(k * LANES, LANES), LANES)
        ft[at, :] = fp[:, at].T
        v = v_ref[k]
        w_ref[k] = lax.dot_general(
            v * sv_ref[0, pl.ds(k, 1), :], v, (((1,), (1,)), ((), ())),
            precision=highest, preferred_element_type=F32,
        ).astype(BF16)

    position = lax.broadcasted_iota(jnp.int32, (kp, 1), 0)
    valid = (position % wide < width) & (position < rows)
    lane = lax.broadcasted_iota(jnp.int32, (8, kp), 1)
    ones = jnp.where((lane % wide < width) & (lane < rows), 1.0, 0.0).astype(BF16)
    low_lane = lax.broadcasted_iota(jnp.int32, (half, LANES), 1) < half
    flat[pl.ds(base, flat.shape[0] - base), :] = jnp.zeros((flat.shape[0] - base, LANES), F32)

    def copy(src, dst, s, t, bit):
        c = pltpu.make_async_remote_copy(
            src_ref=src,
            dst_ref=dst,
            send_sem=send_sem.at[s, t],
            recv_sem=recv_sem.at[s, t],
            device_id=partner(bit),
            device_id_type=pl.DeviceIdType.MESH,
        )
        c.start()
        return c

    sources = [pieces.at[s] for s in range(streams)] + [small]
    buffers = [[scratch[s * bits + t] for t in range(bits)] for s in range(streams + 1)]
    all_orders = [orders[s % 3] for s in range(streams)] + [orders[0]]
    flights = {}

    def begin(s, t):
        bit = all_orders[s][t]
        size = count >> (t + 1)
        src = sources[s] if t == 0 else buffers[s][t - 1]
        flights[s] = copy(
            src.at[pl.ds((1 - bit_of(bit)) * size, size)], buffers[s][t], s, t, bit
        )

    def finish(s, t):
        size = count >> (t + 1)
        src = sources[s] if t == 0 else buffers[s][t - 1]
        dst = buffers[s][t]
        flights[s].wait()
        first = bit_of(all_orders[s][t]) * size

        @pl.loop(0, size)
        def _(i):
            dst[i] = dst[i] + src[first + i]

    slot = slot_of(index, all_orders[streams])

    def spread(u):
        region = pl.ds(slot // 2**u * 2**u, 2**u)
        flights[streams] = copy(
            total.at[region], total.at[region], streams, bits + u,
            all_orders[streams][bits - 1 - u],
        )

    def advance(t):
        if t < bits:
            finish(streams, t)
            if t + 1 < bits:
                begin(streams, t + 1)
            else:
                total[slot] = buffers[streams][t][0]
                spread(0)
        else:
            flights[streams].wait()
            if t + 1 < 2 * bits:
                spread(t + 1 - bits)

    def piece(s):
        high = 4 * LANES

        @pl.loop(0, channels // high)
        def _(m):
            at = pl.ds(pl.multiple_of(m * high, high), high)
            part = jnp.dot(
                ft[at, :],
                cols[:, s * part_width : (s + 1) * part_width],
                preferred_element_type=F32,
            )
            for q in range(4):
                weight = w_ref[4 * m + q]
                block = part[q * LANES : (q + 1) * LANES]
                one = block.astype(BF16)
                left = block - one.astype(F32)
                two = left.astype(BF16)
                three = (left - two.astype(F32)).astype(BF16)
                result = sum(
                    lax.dot_general(
                        weight, x, (((0,), (0,)), ((), ())), preferred_element_type=F32
                    )
                    for x in (one, two, three)
                )
                for j in range(LANES // per):
                    chunk = (4 * m + q) * (LANES // per) + j
                    pieces[s, slot_of(chunk, all_orders[s])] = result[j * per : (j + 1) * per]

    step = 2 * LANES

    def back_part(n):
        at = pl.ds(pl.multiple_of(n * step, step), step)
        grad = jnp.dot(cols[...], k_ref[:, at], preferred_element_type=F32)
        back[:, at] = grad
        summed = jnp.sum(jnp.where(valid, grad, 0.0), axis=0, keepdims=True)
        low = grad.astype(BF16)
        raw = jnp.dot(ft[at, :], low, preferred_element_type=F32)
        fsum = jnp.dot(ones, fp[:, at], preferred_element_type=F32)
        for q in range(2):
            block = raw[q * LANES : (q + 1) * LANES, q * LANES : (q + 1) * LANES]
            where = pl.multiple_of((2 * n + q) * half, half)
            flat[pl.ds(where, half), :] = jnp.where(low_lane, block[:half], block[half:])
            flat[pl.ds(base + 2 * n + q, 1), :] = summed[:, q * LANES : (q + 1) * LANES]
            flat[pl.ds(base + blocks + 2 * n + q, 1), :] = fsum[:1, q * LANES : (q + 1) * LANES]

    def pack_sums():
        colsum = jnp.dot(ones, cols[...], preferred_element_type=F32)
        for q in range(3 * taps // LANES):
            flat[pl.ds(base + 2 * blocks + q, 1), :] = colsum[:1, q * LANES : (q + 1) * LANES]

        @pl.loop(0, count)
        def _(i):
            small[i] = flat[pl.ds(pl.multiple_of(i * rp, 8), rp), :]

    pl.semaphore_wait(barrier, bits)
    for s in range(streams):
        piece(s)
        begin(s, 0)
        if s > 0:
            finish(s - 1, 0)
            begin(s - 1, 1)
    finish(streams - 1, 0)
    begin(streams - 1, 1)
    k_copy.wait()
    turns = channels // step
    pl.loop(0, turns // 2)(back_part)
    for s in range(streams // 2):
        finish(s, 1)
        begin(s, 2)
    pl.loop(turns // 2, turns)(back_part)
    pack_sums()
    begin(streams, 0)
    done = 0
    for t in (1, 2):
        for s in range(streams):
            if t == 2 or s >= streams // 2:
                finish(s, t)
                begin(s, t + 1)
                if done < 2 * bits:
                    advance(done)
                    done += 1
    while done < 2 * bits:
        advance(done)
        done += 1

    @pl.loop(0, count)
    def _(i):
        flat[pl.ds(pl.multiple_of(i * rp, 8), rp), :] = total[i]

    def across(line):
        return jnp.broadcast_to(line, (LANES, LANES)).T

    side = lax.broadcasted_iota(jnp.int32, (LANES, LANES), 0) < half
    other = lax.broadcasted_iota(jnp.int32, (LANES, LANES), 1) < half
    inside = side == other

    @pl.loop(0, blocks)
    def _(k):
        packed = flat[pl.ds(pl.multiple_of(k * half, half), half), :]
        mean = flat[pl.ds(base + blocks + k, 1), :] / pixel_total
        summed = flat[pl.ds(base + k, 1), :]
        raw = jnp.concatenate([packed, packed], axis=0)
        cov = jnp.where(inside, raw - across(mean) * summed, 0.0)
        v = v_ref[k]
        scale = sv_ref[0, pl.ds(k, 1), :]
        root = sv_ref[1, pl.ds(k, 1), :]
        turned = lax.dot_general(
            v, cov, (((0,), (0,)), ((), ())), precision=highest, preferred_element_type=F32
        )
        rotated = jnp.dot(turned, v, precision=highest, preferred_element_type=F32)
        symmetric = 0.5 * (rotated + rotated.T)
        factor = -(across(scale) * scale) / (across(root) + root)
        inner = jnp.where(inside, symmetric * factor, 0.0)
        outer = jnp.dot(v, inner, precision=highest, preferred_element_type=F32)
        sigma = lax.dot_general(
            outer, v, (((1,), (1,)), ((), ())), precision=highest, preferred_element_type=F32
        )
        s_ref[k] = (2.0 / pixel_total * sigma).astype(BF16)

    def final_part(b):
        here = pl.ds(pl.multiple_of(b * image_rows, 16), image_rows)
        for k in range(blocks):
            at = slice(k * LANES, (k + 1) * LANES)
            mean = flat[base + blocks + k : base + blocks + k + 1, :] / pixel_total
            shift = flat[base + k : base + k + 1, :] / pixel_total
            shifted = (back[here, at] - shift).astype(BF16)
            centered = (fp[here, at].astype(F32) - mean).astype(BF16)
            out = jnp.dot(shifted, w_ref[k], preferred_element_type=F32) + jnp.dot(
                centered, s_ref[k], preferred_element_type=F32
            )
            o_ref[b, :, :, at] = out.astype(BF16).reshape(height, wide, LANES)[:, :width]

    pl.loop(0, images // 2)(final_part)
    for s in range(streams):
        finish(s, 3)
        if bits > 4:
            begin(s, 4)
    pl.loop(images // 2, images)(final_part)
    for t in range(4, bits):
        for s in range(streams):
            finish(s, t)
            if t + 1 < bits:
                begin(s, t + 1)

    mine = index * per // LANES
    mean = flat[pl.ds(base + blocks + mine, 1), :] / pixel_total
    whitened = jnp.dot(
        jnp.broadcast_to(mean, (8, LANES)), w_ref[mine].astype(F32),
        precision=highest, preferred_element_type=F32,
    )
    column[...] = across(whitened[:1])
    mean_part = column[pl.ds(pl.multiple_of(index * per % LANES, per), per), :]
    for s in range(streams):
        for q in range(part_width // LANES):
            at = s * (part_width // LANES) + q
            line = flat[base + 2 * blocks + at : base + 2 * blocks + at + 1, :]
            share_ref[:, at * LANES : (at + 1) * LANES] = (
                buffers[s][bits - 1][0, :, q * LANES : (q + 1) * LANES] - mean_part * line
            )


def pair_blocks(blocks):
    groups, size = blocks.shape[:2]
    pairs = blocks.reshape(groups // 2, 2, size, size)
    zero = jnp.zeros((groups // 2, size, size), blocks.dtype)
    top = jnp.concatenate([pairs[:, 0], zero], axis=2)
    bottom = jnp.concatenate([zero, pairs[:, 1]], axis=2)
    return jnp.concatenate([top, bottom], axis=1)


def local(shape, features, grads, kernel, vectors, values):
    images, height, width, channels = features.shape
    outputs = grads.shape[3]
    groups, group_size = values.shape
    devices = shape[0] * shape[1]
    bits = devices.bit_length() - 1
    orders = bit_orders(bits)
    per = channels // devices
    taps = 3 * outputs
    wide = round_up(width, 16)
    rows = images * height * wide
    kp = round_up(rows + 1, LANES)
    blocks = channels // LANES
    pixel_total = 1.0 * images * height * width * devices
    small_rows = channels // 2 + 2 * blocks + 3 * taps // LANES
    rp = round_up(-(-small_rows // devices), 8)

    streams = 6
    part_width = 3 * taps // streams
    lines = jnp.stack([lax.rsqrt(values), jnp.sqrt(values)]).reshape(2, blocks, LANES)
    vmem = pl.BlockSpec(memory_space=pltpu.VMEM)
    scratch = []
    for _ in range(streams):
        scratch += [pltpu.VMEM((devices >> (t + 1), per, part_width), F32) for t in range(bits)]
    scratch += [pltpu.VMEM((devices >> (t + 1), rp, LANES), F32) for t in range(bits)]
    sizes = (
        shape[0], shape[1], images, height, width, wide, channels, outputs, per, orders,
        streams, pixel_total,
    )
    input_grad, share = pl.pallas_call(
        functools.partial(step_kernel, sizes),
        out_shape=(
            jax.ShapeDtypeStruct(features.shape, BF16),
            jax.ShapeDtypeStruct((per, 3 * taps), F32),
        ),
        in_specs=[vmem, vmem, pl.BlockSpec(memory_space=pl.ANY), vmem, vmem],
        out_specs=(vmem, vmem),
        scratch_shapes=[
            pltpu.VMEM((kp, channels), BF16),
            pltpu.VMEM((channels, kp), BF16),
            pltpu.VMEM((kp, 3 * taps), BF16),
            pltpu.VMEM((height + 2, wide + 8, outputs), F32),
            pltpu.VMEM((3 * taps, channels), BF16),
            pltpu.VMEM((kp, channels), F32),
            pltpu.VMEM((blocks, LANES, LANES), BF16),
            pltpu.VMEM((blocks, LANES, LANES), BF16),
            pltpu.VMEM((devices * rp, LANES), F32),
            pltpu.VMEM((devices, rp, LANES), F32),
            pltpu.VMEM((devices, rp, LANES), F32),
            pltpu.VMEM((LANES, LANES), F32),
            pltpu.VMEM((streams, devices, per, part_width), F32),
            pltpu.SemaphoreType.DMA,
            pltpu.SemaphoreType.DMA((streams + 1, 2 * bits)),
            pltpu.SemaphoreType.DMA((streams + 1, 2 * bits)),
        ]
        + scratch,
        compiler_params=pltpu.CompilerParams(
            collective_id=0, has_side_effects=True, vmem_limit_bytes=VMEM_LIMIT
        ),
        name="step",
    )(features, grads, kernel.reshape(3 * taps, channels), pair_blocks(vectors), lines)
    return (input_grad, share.reshape(per, 3, 3, outputs))


def solution(mesh):
    shape = (mesh.shape["batch"], mesh.shape["rows"])
    split = P(("batch", "rows"), None, None, None)
    return jax.shard_map(
        functools.partial(local, shape),
        mesh=mesh,
        in_specs=(split, split, P(), P(), P()),
        out_specs=(split, split),
        check_vma=False,
    )
```

profile of v0, /device:TPU:0, one launch (start us, length us, event | category | flops | bytes accessed | tf_op | source)
XLA Modules:
  0.0 108.0 jit_solution(11618102305228218466)
XLA Ops:
  0.6 0.7 fusion
  1.3 0.1 stack.9
  1.4 0.1 stack.10
  1.5 0.6 pad_maximum_fusion.sv_ref
  2.1 1.1 slice_bitcast_fusion.1
  3.2 0.9 select_maximum_fusion.v_ref
  4.1 98.3 %step.1 = (bf16[6,14,14,1024]{3,2,1,0:T(8,128)(2,1)}, f32[32,2304]{1,0:T(8,128)}) custom-call(bf16[6,14,14,1024]{3,2,1,0:T(8,128)(2,1)} %f_ref.1, bf16[6,14,14,256]{3,2,1,0:T(8,128)(2,1)} %g_ref.1, bf16[2304,1024]{1,0:T(8,128)(2,1)} %bitcast.10, f32[8,128,128]{2,1,0:T(8,128)} %select_maximum_fusion.v_ref, f32[2,8,128]{2,1,0:T(8,128)} %pad_maximum_fusion.sv_ref), custom_call_target="tpu_custom_call" | custom-call | tf_op jit(solution)/shard_map/step/pallas_call | solution.py:367
  102.4 1.1 %reshape.20 = f32[32,3,3,256]{3,2,1,0:T(4,128)S(1)} reshape(f32[32,2304]{1,0:T(8,128)} %get-tuple-element.5) | data formatting | bytes 589824 | tf_op jit(solution)/shard_map/reshape | solution.py:399
  103.5 0.8 copy.10
  104.3 3.8 %copy.14 = bf16[6,14,14,1024]{3,2,1,0:T(8,128)(2,1)} copy(bf16[6,14,14,1024]{3,2,1,0:T(8,128)(2,1)} %get-tuple-element.16) | data formatting | bytes 4816896
where the time goes:
time: 108 us
  Pallas kernels  98.3 us (91%)
  local copies, waits for them, and re-layouts  7.57 us (7%)
  other arithmetic  1.54 us (1%)
    pallas_call x1, Pallas kernels, local(): pl.pallas_call(functools.partial(step_kernel, sizes), out_shape=(jax.Shap...  98.3 us
    unnamed x2, local copies, waits for them, and re-layouts  4.55 us

commit v1 on v0

--- a/solution.py
+++ b/solution.py
@@ -32,7 +32,7 @@
     return slot
 
 
-def step_kernel(
+def general_kernel(
     sizes, f_ref, g_ref, k_hbm, v_ref, sv_ref, o_ref, share_ref,
     fp, ft, cols, gpad, k_ref, back, w_ref, s_ref, flat, small, total, column, pieces,
     k_sem, send_sem, recv_sem, *scratch
@@ -335,7 +335,7 @@
     return jnp.concatenate([top, bottom], axis=1)
 
 
-def local(shape, features, grads, kernel, vectors, values):
+def general_local(shape, features, grads, kernel, vectors, values):
     images, height, width, channels = features.shape
     outputs = grads.shape[3]
     groups, group_size = values.shape
@@ -365,7 +365,7 @@
         streams, pixel_total,
     )
     input_grad, share = pl.pallas_call(
-        functools.partial(step_kernel, sizes),
+        functools.partial(general_kernel, sizes),
         out_shape=(
             jax.ShapeDtypeStruct(features.shape, BF16),
             jax.ShapeDtypeStruct((per, 3 * taps), F32),
@@ -399,11 +399,716 @@
     return (input_grad, share.reshape(per, 3, 3, outputs))
 
 
+PAIR, SHALLOW = 2, 2
+
+
+def plan_kernel(
+    sizes, f_ref, g_ref, k_hbm, v_ref, val_ref, o_ref, share_ref,
+    fp, ft, cols, gpad, k_ref, back, w_ref, own_ref, s_ref, means,
+    parts, swap, near1, near2, zsum, zin, zfar, early_in, early_far, early1, early2,
+    total, mixed, mixed_in, stat, stat_in, stat_far, known, table,
+    k_sem, send_sem, recv_sem
+):
+    (images, height, width, wide, channels, outputs, group, depth, pixel_total) = sizes
+    rows = images * height * wide
+    kp = fp.shape[0]
+    groups = channels // group
+    blocks = channels // LANES
+    tiles = 9
+    taps = 3 * outputs
+    quarter = group // 2
+    plane = groups // depth
+    image_rows = height * wide
+    packed = quarter // 2
+
+    batch = lax.axis_index("batch")
+    row = lax.axis_index("rows")
+    core = row % PAIR
+    x = row // PAIR
+    y = batch % SHALLOW
+    z = batch // SHALLOW
+    chip = (z * SHALLOW + y) * SHALLOW + x
+    znear = z + 1 - 2 * (z % 2)
+    zother = depth - 1 - z
+    outer = (z == 0) | (z == depth - 1)
+    inner = (z > 0) & (z < depth - 1)
+
+    def place(x, y, z, core=core):
+        return (z * SHALLOW + y, x * PAIR + core)
+
+    partner = place(x, y, z, 1 - core)
+    xside = place(1 - x, y, z)
+    yside = place(x, 1 - y, z)
+
+    def peer(k):
+        px = 1 - x if k % 2 else x
+        py = 1 - y if k // 2 % 2 else y
+        low = 1 - z % 2 if k // 4 % 2 else z % 2
+        high = 1 - z // 2 if k // 8 % 2 else z // 2
+        pz = high * 2 + low
+        return px, py, pz
+
+    barrier = pltpu.get_barrier_semaphore()
+    greet = [partner] + [place(*peer(k)) for k in range(1, groups)]
+    for other in greet:
+        pl.semaphore_signal(
+            barrier, inc=1, device_id=other, device_id_type=pl.DeviceIdType.MESH
+        )
+    k_copy = pltpu.make_async_copy(k_hbm, k_ref, k_sem)
+    k_copy.start()
+
+    sems = {}
+
+    def copy(key, src, dst, device, landing=None):
+        at = sems.setdefault(key, len(sems))
+        to = at if landing is None else sems.setdefault(landing, len(sems))
+        return pltpu.make_async_remote_copy(
+            src_ref=src, dst_ref=dst, send_sem=send_sem.at[at], recv_sem=recv_sem.at[to],
+            device_id=device, device_id_type=pl.DeviceIdType.MESH,
+        )
+
+    flights = {}
+
+    def send(key, src, dst, device):
+        flights[key] = copy(key, src, dst, device)
+        flights[key].start()
+
+    def arrive(key):
+        flights.pop(key).wait()
+
+    fp[pl.ds(rows, kp - rows), :] = jnp.zeros((kp - rows, channels), BF16)
+    cols[pl.ds(rows, kp - rows), :] = jnp.zeros((kp - rows, 3 * taps), BF16)
+    gpad[...] = jnp.zeros(gpad.shape, F32)
+
+    @pl.loop(0, images)
+    def _(b):
+        gpad[pl.ds(1, height), pl.ds(1, width), :] = g_ref[b].astype(F32)
+        for h in range(height):
+            at = pl.multiple_of((b * height + h) * wide, 16)
+            fp[pl.ds(at, wide), :] = jnp.zeros((wide, channels), BF16)
+            fp[pl.ds(at, width), :] = f_ref[b, h]
+        at = pl.multiple_of(b * image_rows, 16)
+        for c in range(3):
+            shifted = gpad[:, 2 - c : 2 - c + wide, :].astype(BF16)
+            for a in range(3):
+                first = a * taps + c * outputs
+                cols[pl.ds(at, image_rows), first : first + outputs] = shifted[
+                    2 - a : 2 - a + height
+                ].reshape(image_rows, outputs)
+
+    @pl.loop(0, blocks)
+    def _(k):
+        at = pl.ds(pl.multiple_of(k * LANES, LANES), LANES)
+        ft[at, :] = fp[:, at].T
+
+    position = lax.broadcasted_iota(jnp.int32, (kp, 1), 0)
+    valid = (position % wide < width) & (position < rows)
+    lane = lax.broadcasted_iota(jnp.int32, (16, kp), 1)
+    ft[pl.ds(channels, 16), :] = jnp.where(
+        (lane % wide < width) & (lane < rows), 1.0, 0.0
+    ).astype(BF16)
+    stat[:, :, pl.ds(packed, 8), :] = jnp.zeros((PAIR, groups, 8, LANES), F32)
+
+    first_plane = [0, 2, 4, 5, 6, 7, 8]
+    first_depth = [1, 3]
+
+    def slot(t, half, g):
+        gz, gy, gx = g // 4, g // 2 % 2, g % 2
+        first, second = (gx, gy) if half == 0 else (gy, gx)
+        if t in first_depth:
+            return gz * 4 + first * 2 + second
+        return first * 8 + second * 4 + gz
+
+    def tile(t):
+        high = channels // 2
+        for m in range(2):
+            extra = 16 if m == 1 else 0
+            part = jnp.dot(
+                ft[m * high : (m + 1) * high + extra, :],
+                cols[:, t * outputs : (t + 1) * outputs],
+                preferred_element_type=F32,
+            )
+            for q in range(groups // 2):
+                g = m * (groups // 2) + q
+                for half in range(2):
+                    lines = slice(q * group + half * quarter, q * group + (half + 1) * quarter)
+                    for c in range(PAIR):
+                        parts[t, c, half, slot(t, half, g)] = part[
+                            lines, c * LANES : (c + 1) * LANES
+                        ]
+            if m == 1:
+                for c in range(PAIR):
+                    stat[c, t, packed + 1 : packed + 2, :] = part[
+                        high : high + 1, c * LANES : (c + 1) * LANES
+                    ]
+        send(("swap", t), parts.at[t, 1 - core], swap.at[t], partner)
+
+    def add(dst, src, dst_first, count, src_first=0):
+        @pl.loop(0, count)
+        def _(i):
+            dst[dst_first + i] = dst[dst_first + i] + src[src_first + i]
+
+    def mine(t, half):
+        return parts.at[t, core, half]
+
+    firsts = [(x, y), (y, x)]
+    sides = [(xside, yside), (yside, xside)]
+
+    def swapped(t):
+        arrive(("swap", t))
+        for half in range(2):
+            add(mine(t, half), swap.at[t, half], 0, groups)
+
+    def plane1(t):
+        for half in range(2):
+            send(
+                ("p1", t, half),
+                mine(t, half).at[pl.ds((1 - firsts[half][0]) * 8, 8)],
+                near1.at[t, half], sides[half][0],
+            )
+
+    def plane2(t):
+        for half in range(2):
+            arrive(("p1", t, half))
+            f, s = firsts[half]
+            add(mine(t, half), near1.at[t, half], f * 8 + (1 - s) * 4, 4, (1 - s) * 4)
+            send(
+                ("p2", t, half),
+                mine(t, half).at[pl.ds(f * 8 + (1 - s) * 4, 4)],
+                near2.at[t, half], sides[half][1],
+            )
+        for half in range(2):
+            f, s = firsts[half]
+            add(mine(t, half), near1.at[t, half], f * 8 + s * 4, 4, s * 4)
+
+    def depth1(t):
+        for half in range(2):
+            arrive(("p2", t, half))
+            f, s = firsts[half]
+            src = mine(t, half)
+            for j in range(depth):
+                zsum[t, j, pl.ds(half * quarter, quarter)] = (
+                    src[f * 8 + s * 4 + j] + near2[t, half, j]
+                )
+        key = ("z1", t)
+
+        @pl.when(outer)
+        def _():
+            copy(
+                key, zsum.at[t, pl.ds((depth - 1 - z) // 3, 3)], zin.at[t], place(x, y, znear)
+            ).start()
+
+        @pl.when(inner)
+        def _():
+            copy(
+                key, zsum.at[t, pl.ds(znear, 1)], zin.at[t, pl.ds(0, 1)], place(x, y, znear)
+            ).start()
+
+    def depth2(t):
+        key = ("z1", t)
+
+        @pl.when(outer)
+        def _():
+            near = place(x, y, znear)
+            copy(key, zsum.at[t, pl.ds((depth - 1 - z) // 3, 3)], zin.at[t], near).wait_send()
+            copy(key, zsum.at[t, pl.ds(0, 1)], zin.at[t, pl.ds(0, 1)], near).wait_recv()
+            zsum[t, z] = zsum[t, z] + zin[t, 0]
+
+        @pl.when(inner)
+        def _():
+            near = place(x, y, znear)
+            copy(key, zsum.at[t, pl.ds(znear, 1)], zin.at[t, pl.ds(0, 1)], near).wait_send()
+            copy(key, zsum.at[t, pl.ds(0, 3)], zin.at[t], near).wait_recv()
+            for j in range(3):
+                zsum[t, 2 - z + j] = zsum[t, 2 - z + j] + zin[t, j]
+            copy(
+                ("z2", t), zsum.at[t, pl.ds(zother, 1)], zfar.at[t], place(x, y, zother)
+            ).start()
+            zfin = 3 * (2 - z)
+            copy(
+                ("z3", t), zsum.at[t, pl.ds(zfin, 1)], zfar.at[t], place(x, y, zfin), ("z2", t)
+            ).start()
+
+    def depth3(t):
+        @pl.when(inner)
+        def _():
+            copy(
+                ("z2", t), zsum.at[t, pl.ds(zother, 1)], zfar.at[t], place(x, y, zother)
+            ).wait_send()
+            zfin = 3 * (2 - z)
+            copy(
+                ("z3", t), zsum.at[t, pl.ds(zfin, 1)], zfar.at[t], place(x, y, zfin), ("z2", t)
+            ).wait_send()
+
+        copy(
+            ("z2", t), zsum.at[t, pl.ds(0, 1)], zfar.at[t], place(x, y, zother)
+        ).wait_recv()
+        total[t] = zsum[t, z] + zfar[t, 0]
+
+    def early1_start(t, half):
+        e = first_depth.index(t)
+        key = ("e1", t, half)
+        src = mine(t, half)
+
+        @pl.when(outer)
+        def _():
+            copy(
+                key, src.at[pl.ds((depth - 1 - z) // 3 * 4, 12)], early_in.at[e, half],
+                place(x, y, znear),
+            ).start()
+
+        @pl.when(inner)
+        def _():
+            copy(
+                key, src.at[pl.ds(znear * 4, 4)], early_in.at[e, half, pl.ds(0, 4)],
+                place(x, y, znear),
+            ).start()
+
+    def early2_start(t, half):
+        e = first_depth.index(t)
+        key = ("e1", t, half)
+        src = mine(t, half)
+        buf = early_in.at[e, half]
+        far = early_far.at[e, half]
+
+        @pl.when(outer)
+        def _():
+            near = place(x, y, znear)
+            copy(key, src.at[pl.ds((depth - 1 - z) // 3 * 4, 12)], buf, near).wait_send()
+            copy(key, src.at[pl.ds(0, 4)], buf.at[pl.ds(0, 4)], near).wait_recv()
+            add(src, buf, z * 4, 4)
+
+        @pl.when(inner)
+        def _():
+            near = place(x, y, znear)
+            copy(key, src.at[pl.ds(znear * 4, 4)], buf.at[pl.ds(0, 4)], near).wait_send()
+            copy(key, src.at[pl.ds(0, 12)], buf, near).wait_recv()
+            add(src, buf, (2 - z) * 4, 12)
+            copy(
+                ("e2", t, half), src.at[pl.ds(zother * 4, 4)], far, place(x, y, zother)
+            ).start()
+            zfin = 3 * (2 - z)
+            copy(
+                ("e3", t, half), src.at[pl.ds(zfin * 4, 4)], far, place(x, y, zfin),
+                ("e2", t, half),
+            ).start()
+
+    def early3_start(t, half):
+        e = first_depth.index(t)
+        src = mine(t, half)
+        far = early_far.at[e, half]
+
+        @pl.when(inner)
+        def _():
+            copy(
+                ("e2", t, half), src.at[pl.ds(zother * 4, 4)], far, place(x, y, zother)
+            ).wait_send()
+            zfin = 3 * (2 - z)
+            copy(
+                ("e3", t, half), src.at[pl.ds(zfin * 4, 4)], far, place(x, y, zfin),
+                ("e2", t, half),
+            ).wait_send()
+
+        copy(("e2", t, half), src.at[pl.ds(0, 4)], far, place(x, y, zother)).wait_recv()
+        add(src, far, z * 4, 4)
+        send(
+            ("e4", t, half),
+            src.at[pl.ds(z * 4 + (1 - firsts[half][0]) * 2, 2)],
+            early1.at[e, half], sides[half][0],
+        )
+
+    def early4_start(t, half):
+        e = first_depth.index(t)
+        arrive(("e4", t, half))
+        f, s = firsts[half]
+        src = mine(t, half)
+        add(src, early1.at[e, half], z * 4 + f * 2, 2)
+        send(
+            ("e5", t, half),
+            src.at[pl.ds(z * 4 + f * 2 + (1 - s), 1)],
+            early2.at[e, half], sides[half][1],
+        )
+
+    def early5(t, half):
+        e = first_depth.index(t)
+        arrive(("e5", t, half))
+        f, s = firsts[half]
+        src = mine(t, half)
+        total[t, pl.ds(half * quarter, quarter)] = (
+            src[z * 4 + f * 2 + s] + early2[e, half, 0]
+        )
+
+    step = 2 * LANES
+    half_rows = kp // 2
+    low_lane = lax.broadcasted_iota(jnp.int32, (quarter, LANES), 1) < LANES // 2
+    low_line = lax.broadcasted_iota(jnp.int32, (8, LANES), 1) < LANES // 2
+
+    def turn(a):
+        return pltpu.roll(a, LANES // 2, 1)
+
+    def back_part(n, r):
+        at = slice(n * step, (n + 1) * step)
+        here = slice(r * half_rows, (r + 1) * half_rows)
+        back[here, at] = jnp.dot(cols[here, :], k_ref[:, at], preferred_element_type=F32)
+
+    def cov_part(n):
+        at = slice(n * step, (n + 1) * step)
+        grad = back[:, at]
+        summed = jnp.broadcast_to(
+            jnp.sum(jnp.where(valid, grad, 0.0), axis=0, keepdims=True), (8, step)
+        )
+        raw = jnp.dot(ft[at, :], grad.astype(BF16), preferred_element_type=F32)
+        fsum = jnp.dot(ft[channels : channels + 16, :], fp[:, at], preferred_element_type=F32)[:8]
+        for q in range(2):
+            wide_at = slice(q * LANES, (q + 1) * LANES)
+            block = raw[wide_at, wide_at]
+            bs, fs = summed[:, wide_at], fsum[:, wide_at]
+            g = (2 * n + q) * 2
+            pieces = [block[i * quarter : (i + 1) * quarter] for i in range(4)]
+            lower = jnp.where(low_lane, pieces[0], turn(pieces[1]))
+            upper = jnp.where(low_lane, turn(pieces[2]), pieces[3])
+            for c in range(PAIR):
+                stat[c, g, :packed] = lower[c * packed : (c + 1) * packed]
+                stat[c, g + 1, :packed] = upper[c * packed : (c + 1) * packed]
+            stat[0, g, packed : packed + 1] = jnp.where(low_line, fs, turn(bs))[:1]
+            stat[0, g + 1, packed : packed + 1] = jnp.where(low_line, turn(fs), bs)[:1]
+
+    def stat1():
+        send("s1", stat.at[1 - core], stat_in, partner)
+
+    def stat2():
+        arrive("s1")
+        src = stat.at[core]
+        add(src, stat_in, 0, groups)
+        for k in range(1, groups):
+            px, py, pz = peer(k)
+            send(
+                ("s2", k), src.at[(pz * SHALLOW + py) * SHALLOW + px], stat_far.at[k],
+                place(px, py, pz),
+            )
+
+    def stat3():
+        summed = stat[core, chip]
+        for k in range(1, groups):
+            arrive(("s2", k))
+            summed = summed + stat_far[k]
+        known[core] = summed
+        send("s3", known.at[core], known.at[core], partner)
+
+    def across(line):
+        return jnp.broadcast_to(line, (LANES, LANES)).T[:group, :group]
+
+    def hdot(a, b, dims):
+        return lax.dot_general(
+            a, b, (dims, ((), ())), precision=highest, preferred_element_type=F32
+        )
+
+    def stat4():
+        arrive("s3")
+        lines = jnp.concatenate([known[0, :packed], known[1, :packed]], axis=0)
+        raw = jnp.concatenate([lines, turn(lines)], axis=0)[:, :group]
+        both = jnp.broadcast_to(known[0, packed : packed + 1], (8, LANES))
+        mean = both[:1] / pixel_total
+        summed = turn(both)[:1, :group]
+        cov = raw - across(mean) * summed
+        v = v_ref[chip]
+        vals = jnp.concatenate(
+            [val_ref[pl.ds(chip, 1), :], jnp.ones((1, LANES - group), F32)], axis=1
+        )
+        scale = lax.rsqrt(vals)
+        root = jnp.sqrt(vals)
+        turned = hdot(v, cov, ((0,), (0,)))
+        rotated = hdot(turned, v, ((1,), (0,)))
+        symmetric = 0.5 * (rotated + rotated.T)
+        factor = -(across(scale) * scale[:, :group]) / (across(root) + root[:, :group])
+        inside = hdot(v, symmetric * factor, ((1,), (0,)))
+        sigma = 2.0 / pixel_total * hdot(inside, v, ((1,), (1,)))
+        own_ref[...] = hdot(v * scale[:, :group], v, ((1,), (1,))).astype(BF16)
+        sigma = jnp.concatenate([sigma, jnp.zeros((group, LANES - group), F32)], axis=1)
+        folded = jnp.where(low_lane, sigma[:quarter], turn(sigma[quarter:]))
+        table[core, chip, :packed] = jnp.where(core == 0, folded[:packed], folded[packed:])
+        table[core, chip, packed:] = known[core, packed:]
+        table[core, chip, packed : packed + 1] = known[0, packed : packed + 1]
+        src = table.at[core, chip]
+        for k in range(1, groups):
+            send(("s4", k), src, src, place(*peer(k)))
+
+    def stat5():
+        for k in range(1, groups):
+            arrive(("s4", k))
+        send("s5", table.at[core], table.at[core], partner)
+
+    def stat6():
+        arrive("s5")
+        for k in range(blocks):
+            folded = [
+                jnp.concatenate([table[0, 2 * k + q, :packed], table[1, 2 * k + q, :packed]], axis=0)
+                for q in range(2)
+            ]
+            s_ref[k] = jnp.concatenate(
+                [
+                    jnp.where(low_lane, folded[0], 0.0),
+                    jnp.where(low_lane, turn(folded[0]), 0.0),
+                    jnp.where(low_lane, 0.0, turn(folded[1])),
+                    jnp.where(low_lane, 0.0, folded[1]),
+                ],
+                axis=0,
+            ).astype(BF16)
+            sums = [
+                jnp.broadcast_to(table[0, 2 * k + q, packed : packed + 1], (8, LANES))
+                for q in range(2)
+            ]
+            means[0, k] = jnp.where(low_line, sums[0], turn(sums[1])) / pixel_total
+            means[1, k] = jnp.where(low_line, turn(sums[0]), sums[1]) / pixel_total
+
+    def whiten_part(k):
+        zero = jnp.zeros((group, LANES - group), F32)
+        for q in range(2):
+            g = 2 * k + q
+            v = v_ref[g]
+            scaled = v * lax.rsqrt(val_ref[g : g + 1, :])
+            w = jnp.concatenate([hdot(scaled, v, ((1,), (1,))), zero], axis=1)
+            if q == 1:
+                w = turn(w)
+            w_ref[k, q * group : (q + 1) * group, :] = w.astype(BF16)
+
+    def final_part(b):
+        here = pl.ds(pl.multiple_of(b * image_rows, 16), image_rows)
+        for k in range(blocks):
+            at = slice(k * LANES, (k + 1) * LANES)
+            shifted = (back[here, at] - means[1, k, :1]).astype(BF16)
+            centered = (fp[here, at].astype(F32) - means[0, k, :1]).astype(BF16)
+            out = jnp.dot(shifted, w_ref[k], preferred_element_type=F32) + jnp.dot(
+                centered, s_ref[k], preferred_element_type=F32
+            )
+            o_ref[b, :, :, at] = out.astype(BF16).reshape(height, wide, LANES)[:, :width]
+
+    def whitened(t):
+        both = known[0, packed : packed + 1] / pixel_total
+        mean = jnp.broadcast_to(both, (LANES, LANES)).T[:group]
+        block = total[t] - mean * table[core, t, packed + 1 : packed + 2]
+        one = block.astype(BF16)
+        left = block - one.astype(F32)
+        two = left.astype(BF16)
+        three = (left - two.astype(F32)).astype(BF16)
+        weight = own_ref[...]
+        mixed[t] = sum(
+            lax.dot_general(weight, a, (((0,), (0,)), ((), ())), preferred_element_type=F32)
+            for a in (one, two, three)
+        )
+        send(("m", t), mixed.at[t, pl.ds((1 - core) * quarter, quarter)], mixed_in.at[t], partner)
+        here = pl.ds(pl.multiple_of(core * LANES, LANES), LANES)
+        share_ref[t, :, here] = mixed[t, pl.ds(core * quarter, quarter)]
+
+    def finished(t):
+        arrive(("m", t))
+        there = pl.ds(pl.multiple_of((1 - core) * LANES, LANES), LANES)
+        share_ref[t, :, there] = mixed_in[t]
+
+    p = first_plane
+    e = first_depth
+    early = [(t, half) for t in e for half in range(2)]
+    pl.semaphore_wait(barrier, len(greet))
+    tile(p[0])
+    tile(e[0])
+    tile(p[1])
+    swapped(p[0])
+    plane1(p[0])
+    tile(e[1])
+    swapped(e[0])
+    early1_start(*early[0])
+    early1_start(*early[1])
+    tile(p[2])
+    swapped(p[1])
+    plane1(p[1])
+    tile(p[3])
+    swapped(e[1])
+    early1_start(*early[2])
+    early1_start(*early[3])
+    tile(p[4])
+    swapped(p[2])
+    plane1(p[2])
+    tile(p[5])
+    swapped(p[3])
+    plane2(p[0])
+    plane1(p[3])
+    tile(p[6])
+    swapped(p[4])
+    k_copy.wait()
+    back_part(0, 0)
+    swapped(p[5])
+    back_part(0, 1)
+    early2_start(*early[0])
+    plane2(p[1])
+    plane1(p[4])
+    cov_part(0)
+    swapped(p[6])
+    back_part(1, 0)
+    back_part(1, 1)
+    plane2(p[2])
+    plane1(p[5])
+    early2_start(*early[1])
+    cov_part(1)
+    depth1(p[0])
+    back_part(2, 0)
+    early3_start(*early[0])
+    back_part(2, 1)
+    plane2(p[3])
+    plane1(p[6])
+    cov_part(2)
+    early2_start(*early[2])
+    back_part(3, 0)
+    depth1(p[1])
+    back_part(3, 1)
+    plane2(p[4])
+    cov_part(3)
+    stat1()
+    early3_start(*early[1])
+    whiten_part(0)
+    whiten_part(1)
+    stat2()
+    early2_start(*early[3])
+    depth1(p[2])
+    for k in range(2, blocks):
+        whiten_part(k)
+    plane2(p[5])
+    early4_start(*early[0])
+    early4_start(*early[1])
+    depth2(p[0])
+    stat3()
+    early3_start(*early[2])
+    stat4()
+    depth1(p[3])
+    depth2(p[1])
+    plane2(p[6])
+    early5(*early[0])
+    early5(*early[1])
+    early3_start(*early[3])
+    depth2(p[2])
+    depth1(p[4])
+    depth3(p[0])
+    depth3(p[1])
+    stat5()
+    early4_start(*early[2])
+    early4_start(*early[3])
+    depth2(p[3])
+    depth1(p[5])
+    stat6()
+    depth3(p[2])
+    pl.loop(0, images // 3)(final_part)
+    depth1(p[6])
+    depth2(p[4])
+    depth3(p[3])
+    pl.loop(images // 3, 2 * images // 3)(final_part)
+    early5(*early[2])
+    early5(*early[3])
+    depth2(p[5])
+    depth3(p[4])
+    pl.loop(2 * images // 3, images)(final_part)
+    for t in (e[0], e[1], p[0], p[1], p[2], p[3], p[4]):
+        whitened(t)
+    depth2(p[6])
+    depth3(p[5])
+    whitened(p[5])
+    for t in (e[0], e[1], p[0], p[1], p[2], p[3], p[4]):
+        finished(t)
+    depth3(p[6])
+    whitened(p[6])
+    finished(p[5])
+    finished(p[6])
+
+
+def plan_local(shape, features, grads, kernel, vectors, values):
+    images, height, width, channels = features.shape
+    outputs = grads.shape[3]
+    groups, group = values.shape
+    devices = shape[0] * shape[1]
+    depth = shape[0] // SHALLOW
+    taps = 3 * outputs
+    wide = round_up(width, 16)
+    rows = images * height * wide
+    kp = round_up(rows + 1, LANES)
+    blocks = channels // LANES
+    pixel_total = 1.0 * images * height * width * devices
+    quarter = group // 2
+    stat_rows = quarter // 2 + 8
+    sizes = (images, height, width, wide, channels, outputs, group, depth, pixel_total)
+    vmem = pl.BlockSpec(memory_space=pltpu.VMEM)
+    sem_count = 192
+    f32 = [
+        (9, PAIR, 2, groups, quarter, LANES),
+        (9, 2, groups, quarter, LANES),
+        (9, 2, 8, quarter, LANES),
+        (9, 2, 4, quarter, LANES),
+        (9, depth, group, LANES),
+        (9, 3, group, LANES),
+        (9, 1, group, LANES),
+        (2, 2, 12, quarter, LANES),
+        (2, 2, 4, quarter, LANES),
+        (2, 2, 2, quarter, LANES),
+        (2, 2, 1, quarter, LANES),
+        (9, group, LANES),
+        (9, group, LANES),
+        (9, quarter, LANES),
+        (PAIR, groups, stat_rows, LANES),
+        (groups, stat_rows, LANES),
+        (groups, stat_rows, LANES),
+        (PAIR, stat_rows, LANES),
+        (PAIR, groups, stat_rows, LANES),
+    ]
+    input_grad, share = pl.pallas_call(
+        functools.partial(plan_kernel, sizes),
+        out_shape=(
+            jax.ShapeDtypeStruct(features.shape, BF16),
+            jax.ShapeDtypeStruct((9, channels // devices, outputs), F32),
+        ),
+        in_specs=[vmem, vmem, pl.BlockSpec(memory_space=pl.ANY), vmem, vmem],
+        out_specs=(vmem, vmem),
+        scratch_shapes=[
+            pltpu.VMEM((kp, channels), BF16),
+            pltpu.VMEM((channels + 16, kp), BF16),
+            pltpu.VMEM((kp, 3 * taps), BF16),
+            pltpu.VMEM((height + 2, wide + 8, outputs), F32),
+            pltpu.VMEM((3 * taps, channels), BF16),
+            pltpu.VMEM((kp, channels), F32),
+            pltpu.VMEM((blocks, LANES, LANES), BF16),
+            pltpu.VMEM((group, group), BF16),
+            pltpu.VMEM((blocks, LANES, LANES), BF16),
+            pltpu.VMEM((2, blocks, 8, LANES), F32),
+        ]
+        + [pltpu.VMEM(s, F32) for s in f32]
+        + [
+            pltpu.SemaphoreType.DMA,
+            pltpu.SemaphoreType.DMA((sem_count,)),
+            pltpu.SemaphoreType.DMA((sem_count,)),
+        ],
+        compiler_params=pltpu.CompilerParams(
+            collective_id=0, has_side_effects=True, vmem_limit_bytes=VMEM_LIMIT
+        ),
+        name="step",
+    )(features, grads, kernel.reshape(3 * taps, channels), vectors, values)
+    per = channels // devices
+    return (input_grad, share.reshape(3, 3, per, outputs).transpose(2, 0, 1, 3))
+
+
 def solution(mesh):
     shape = (mesh.shape["batch"], mesh.shape["rows"])
     split = P(("batch", "rows"), None, None, None)
+
+    def local(features, grads, kernel, vectors, values):
+        groups, group = values.shape
+        fits = (
+            shape == (SHALLOW * 4, PAIR * SHALLOW)
+            and groups * PAIR == shape[0] * shape[1]
+            and group * 2 == LANES
+            and grads.shape[3] == PAIR * LANES
+            and features.shape[0] % 3 == 0
+        )
+        body = plan_local if fits else general_local
+        return body(shape, features, grads, kernel, vectors, values)
+
     return jax.shard_map(
-        functools.partial(local, shape),
+        local,
         mesh=mesh,
         in_specs=(split, split, P(), P(), P()),
         out_specs=(split, split),

time: 108 us -> 77.4 us (0.72)
  Pallas kernels: 98.3 us -> 72 us
  local copies, waits for them, and re-layouts: 7.57 us -> 4.55 us
  other arithmetic: 1.54 us -> 0 us
    pallas_call x1, Pallas kernels: 98.3 us -> 72 us  [plan_local(): pl.pallas_call(functools.partial(plan_kernel, sizes), out_shape=(jax.Shap...]
    reshape x1 -> x0, local copies, waits for them, and re-layouts: 1.11 us -> none  [local(): return (input_grad, share.reshape(per, 3, 3, outputs))]
    unnamed x2 -> x4, local copies, waits for them, and re-layouts: 4.55 us -> 4.55 us
where the time goes in v1:
time: 77.4 us; the launch traced here: 77.2 us
  Pallas kernels  72 us (93%)
  local copies, waits for them, and re-layouts  4.55 us (6%)
    pallas_call x1, Pallas kernels, plan_local(): pl.pallas_call(functools.partial(plan_kernel, sizes), out_shape=(jax.Shap...  72 us
    unnamed x4, local copies, waits for them, and re-layouts  4.55 us

profile of v1, /device:TPU:0, one launch (start us, length us, event | category | flops | bytes accessed | tf_op | source)
XLA Modules:
  0.0 77.2 jit_solution(7365708621392719490)
XLA Ops:
  0.6 72.0 %step.1 = (bf16[6,14,14,1024]{3,2,1,0:T(8,128)(2,1)}, f32[9,32,256]{2,1,0:T(8,128)}) custom-call(bf16[6,14,14,1024]{3,2,1,0:T(8,128)(2,1)} %f_ref.1, bf16[6,14,14,256]{3,2,1,0:T(8,128)(2,1)} %g_ref.1, bf16[2304,1024]{1,0:T(8,128)(2,1)} %bitcast.4, f32[16,64,64]{2,1,0:T(8,128)} %v_ref.1, f32[16,64]{1,0:T(8,128)} %val_ref.1), custom_call_target="tpu_custom_call" | custom-call | tf_op jit(solution)/shard_map/step/pallas_call | solution.py:1059
  72.6 0.0 copy-start
  72.6 3.8 %copy.9 = bf16[6,14,14,1024]{3,2,1,0:T(8,128)(2,1)} copy(bf16[6,14,14,1024]{3,2,1,0:T(8,128)(2,1)} %get-tuple-element.8) | data formatting | bytes 4816896
  76.5 0.0 copy-done
  76.5 0.7 copy.10
Async XLA Ops:
  72.6 3.8 %copy-start = (f32[9,32,256]{2,1,0:T(8,128)S(1)}, f32[9,32,256]{2,1,0:T(8,128)}, u32[]{:S(2)}) copy-start(f32[9,32,256]{2,1,0:T(8,128)} %get-tuple-element.5) | copy-start | bytes 884740

commit v2 on v1

--- a/solution.py
+++ b/solution.py
@@ -407,7 +407,7 @@
     fp, ft, cols, gpad, k_ref, back, w_ref, own_ref, s_ref, means,
     parts, swap, near1, near2, zsum, zin, zfar, early_in, early_far, early1, early2,
     total, mixed, mixed_in, stat, stat_in, stat_far, known, table,
-    k_sem, send_sem, recv_sem
+    k_sem, send_sem, recv_sem, ready
 ):
     (images, height, width, wide, channels, outputs, group, depth, pixel_total) = sizes
     rows = images * height * wide
@@ -449,11 +449,29 @@
         return px, py, pz
 
     barrier = pltpu.get_barrier_semaphore()
-    greet = [partner] + [place(*peer(k)) for k in range(1, groups)]
-    for other in greet:
-        pl.semaphore_signal(
-            barrier, inc=1, device_id=other, device_id_type=pl.DeviceIdType.MESH
-        )
+    mesh_id = pl.DeviceIdType.MESH
+    near = [xside, yside, place(x, y, znear)]
+    count = len(near) + inner.astype(jnp.int32)
+
+    def tell(sem, devices):
+        for other in devices:
+            pl.semaphore_signal(sem, inc=1, device_id=other, device_id_type=mesh_id)
+
+        @pl.when(inner)
+        def _():
+            pl.semaphore_signal(
+                sem, inc=1, device_id=place(x, y, zother), device_id_type=mesh_id
+            )
+
+    def spread(k):
+        if k > 0:
+            pl.semaphore_wait(ready.at[k - 1], count)
+        tell(ready.at[k], near)
+
+    def spread_done():
+        pl.semaphore_wait(ready.at[3], count)
+
+    tell(barrier, near + [partner])
     k_copy = pltpu.make_async_copy(k_hbm, k_ref, k_sem)
     k_copy.start()
 
@@ -907,114 +925,135 @@
 
     p = first_plane
     e = first_depth
-    early = [(t, half) for t in e for half in range(2)]
-    pl.semaphore_wait(barrier, len(greet))
+    pl.semaphore_wait(barrier, count + 1)
+    spread(0)
     tile(p[0])
+    spread(1)
     tile(e[0])
+    spread(2)
     tile(p[1])
+    spread(3)
+    tile(e[1])
+    spread_done()
     swapped(p[0])
     plane1(p[0])
-    tile(e[1])
+    tile(p[2])
     swapped(e[0])
-    early1_start(*early[0])
-    early1_start(*early[1])
-    tile(p[2])
     swapped(p[1])
     plane1(p[1])
+    early1_start(e[0], 0)
+    early1_start(e[0], 1)
     tile(p[3])
     swapped(e[1])
-    early1_start(*early[2])
-    early1_start(*early[3])
+    early1_start(e[1], 0)
+    early1_start(e[1], 1)
     tile(p[4])
     swapped(p[2])
     plane1(p[2])
     tile(p[5])
     swapped(p[3])
-    plane2(p[0])
     plane1(p[3])
     tile(p[6])
+    plane2(p[0])
     swapped(p[4])
     k_copy.wait()
     back_part(0, 0)
-    swapped(p[5])
     back_part(0, 1)
-    early2_start(*early[0])
-    plane2(p[1])
+    early2_start(e[0], 0)
+    cov_part(0)
     plane1(p[4])
-    cov_part(0)
-    swapped(p[6])
     back_part(1, 0)
     back_part(1, 1)
     plane2(p[2])
-    plane1(p[5])
-    early2_start(*early[1])
     cov_part(1)
-    depth1(p[0])
     back_part(2, 0)
-    early3_start(*early[0])
+    early2_start(e[0], 1)
     back_part(2, 1)
     plane2(p[3])
-    plane1(p[6])
     cov_part(2)
-    early2_start(*early[2])
     back_part(3, 0)
-    depth1(p[1])
+    depth1(p[0])
     back_part(3, 1)
-    plane2(p[4])
+    early2_start(e[1], 0)
     cov_part(3)
     stat1()
-    early3_start(*early[1])
+    whiten_part(7)
+    plane2(p[4])
+    early3_start(e[0], 1)
+    whiten_part(5)
     whiten_part(0)
     whiten_part(1)
+    whiten_part(6)
     stat2()
-    early2_start(*early[3])
     depth1(p[2])
-    for k in range(2, blocks):
-        whiten_part(k)
+    early3_start(e[0], 0)
+    plane2(p[1])
+    whiten_part(3)
+    whiten_part(4)
+    early2_start(e[1], 1)
+    depth1(p[3])
+    swapped(p[5])
+    plane1(p[5])
+    swapped(p[6])
+    whiten_part(2)
+    early3_start(e[1], 0)
+    depth1(p[4])
+    depth2(p[0])
+    early4_start(e[0], 1)
+    plane1(p[6])
+    early4_start(e[0], 0)
+    depth1(p[1])
+    depth2(p[2])
+    early3_start(e[1], 1)
+    stat3()
     plane2(p[5])
-    early4_start(*early[0])
-    early4_start(*early[1])
-    depth2(p[0])
-    stat3()
-    early3_start(*early[2])
+    early4_start(e[1], 0)
     stat4()
-    depth1(p[3])
+    depth2(p[3])
+    depth3(p[0])
+    depth3(p[2])
+    depth2(p[4])
+    early5(e[0], 0)
+    early5(e[0], 1)
+    plane2(p[6])
+    early4_start(e[1], 1)
     depth2(p[1])
-    plane2(p[6])
-    early5(*early[0])
-    early5(*early[1])
-    early3_start(*early[3])
-    depth2(p[2])
-    depth1(p[4])
-    depth3(p[0])
+    depth1(p[5])
+    early5(e[1], 0)
+    early5(e[1], 1)
+    depth1(p[6])
+    depth3(p[3])
+    depth2(p[5])
+    stat5()
+    depth3(p[4])
     depth3(p[1])
-    stat5()
-    early4_start(*early[2])
-    early4_start(*early[3])
-    depth2(p[3])
-    depth1(p[5])
     stat6()
-    depth3(p[2])
-    pl.loop(0, images // 3)(final_part)
-    depth1(p[6])
-    depth2(p[4])
-    depth3(p[3])
-    pl.loop(images // 3, 2 * images // 3)(final_part)
-    early5(*early[2])
-    early5(*early[3])
-    depth2(p[5])
-    depth3(p[4])
-    pl.loop(2 * images // 3, images)(final_part)
-    for t in (e[0], e[1], p[0], p[1], p[2], p[3], p[4]):
-        whitened(t)
+    whitened(p[2])
     depth2(p[6])
+    whitened(p[4])
+    final_part(1)
+    final_part(3)
     depth3(p[5])
     whitened(p[5])
-    for t in (e[0], e[1], p[0], p[1], p[2], p[3], p[4]):
-        finished(t)
+    final_part(5)
+    whitened(p[1])
+    whitened(e[1])
+    whitened(e[0])
+    finished(p[2])
+    whitened(p[0])
+    finished(p[5])
+    final_part(0)
+    whitened(p[3])
+    finished(p[1])
     depth3(p[6])
     whitened(p[6])
-    finished(p[5])
+    finished(e[0])
+    finished(e[1])
+    final_part(4)
+    finished(p[0])
+    final_part(2)
+    finished(p[3])
+    finished(p[4])
     finished(p[6])
 
 
@@ -1081,6 +1120,7 @@
             pltpu.SemaphoreType.DMA,
             pltpu.SemaphoreType.DMA((sem_count,)),
             pltpu.SemaphoreType.DMA((sem_count,)),
+            pltpu.SemaphoreType.REGULAR((4,)),
         ],
         compiler_params=pltpu.CompilerParams(
             collective_id=0, has_side_effects=True, vmem_limit_bytes=VMEM_LIMIT

time: 77.4 us -> 71.2 us (0.920)
  Pallas kernels: 72 us -> 65.9 us
    pallas_call x1, Pallas kernels: 72 us -> 65.9 us  [plan_local(): pl.pallas_call(functools.partial(plan_kernel, sizes), out_shape=(jax.Shap...]
where the time goes in v2:
time: 71.2 us; the launch traced here: 71.1 us
  Pallas kernels  65.9 us (93%)
  local copies, waits for them, and re-layouts  4.55 us (6%)
    pallas_call x1, Pallas kernels, plan_local(): pl.pallas_call(functools.partial(plan_kernel, sizes), out_shape=(jax.Shap...  65.9 us
    unnamed x4, local copies, waits for them, and re-layouts  4.55 us

profile of v2, /device:TPU:0, one launch (start us, length us, event | category | flops | bytes accessed | tf_op | source)
XLA Modules:
  0.0 71.1 jit_solution(2202050068496997214)
XLA Ops:
  0.6 65.9 %step.1 = (bf16[6,14,14,1024]{3,2,1,0:T(8,128)(2,1)}, f32[9,32,256]{2,1,0:T(8,128)}) custom-call(bf16[6,14,14,1024]{3,2,1,0:T(8,128)(2,1)} %f_ref.1, bf16[6,14,14,256]{3,2,1,0:T(8,128)(2,1)} %g_ref.1, bf16[2304,1024]{1,0:T(8,128)(2,1)} %bitcast.4, f32[16,64,64]{2,1,0:T(8,128)} %v_ref.1, f32[16,64]{1,0:T(8,128)} %val_ref.1), custom_call_target="tpu_custom_call" | custom-call | tf_op jit(solution)/shard_map/step/pallas_call | solution.py:1098
  66.5 0.0 copy-start
  66.5 3.8 %copy.9 = bf16[6,14,14,1024]{3,2,1,0:T(8,128)(2,1)} copy(bf16[6,14,14,1024]{3,2,1,0:T(8,128)(2,1)} %get-tuple-element.8) | data formatting | bytes 4816896
  70.4 0.0 copy-done
  70.4 0.7 %copy.10 = f32[32,3,3,256]{3,0,2,1:T(8,128)} copy(f32[32,3,3,256]{3,0,2,1:T(8,128)S(1)} %bitcast.5) | data formatting | bytes 589824
Async XLA Ops:
  66.5 3.8 %copy-start = (f32[9,32,256]{2,1,0:T(8,128)S(1)}, f32[9,32,256]{2,1,0:T(8,128)}, u32[]{:S(2)}) copy-start(f32[9,32,256]{2,1,0:T(8,128)} %get-tuple-element.5) | copy-start | bytes 884740

commit v3 on v2

--- a/solution.py
+++ b/solution.py
@@ -403,11 +403,12 @@
 
 
 def plan_kernel(
-    sizes, f_ref, g_ref, k_hbm, v_ref, val_ref, o_ref, share_ref,
+    sizes, f_hbm, g_hbm, k_hbm, v_hbm, val_hbm, o_hbm, share_hbm,
+    f_ref, g_ref, v_ref, val_ref, o_ref, share_ref,
     fp, ft, cols, gpad, k_ref, back, w_ref, own_ref, s_ref, means,
     parts, swap, near1, near2, zsum, zin, zfar, early_in, early_far, early1, early2,
     total, mixed, mixed_in, stat, stat_in, stat_far, known, table,
-    k_sem, send_sem, recv_sem, ready
+    k_sem, f_sem, o_sem, send_sem, recv_sem, ready
 ):
     (images, height, width, wide, channels, outputs, group, depth, pixel_total) = sizes
     rows = images * height * wide
@@ -473,7 +474,12 @@
 
     tell(barrier, near + [partner])
     k_copy = pltpu.make_async_copy(k_hbm, k_ref, k_sem)
-    k_copy.start()
+    g_copy = pltpu.make_async_copy(g_hbm, g_ref, f_sem.at[0])
+    f_copy = pltpu.make_async_copy(f_hbm, f_ref, f_sem.at[1])
+    v_copy = pltpu.make_async_copy(v_hbm, v_ref, f_sem.at[2])
+    val_copy = pltpu.make_async_copy(val_hbm, val_ref, f_sem.at[3])
+    for load in (g_copy, f_copy, v_copy, val_copy):
+        load.start()
 
     sems = {}
 
@@ -498,13 +504,11 @@
     cols[pl.ds(rows, kp - rows), :] = jnp.zeros((kp - rows, 3 * taps), BF16)
     gpad[...] = jnp.zeros(gpad.shape, F32)
 
+    g_copy.wait()
+
     @pl.loop(0, images)
     def _(b):
         gpad[pl.ds(1, height), pl.ds(1, width), :] = g_ref[b].astype(F32)
-        for h in range(height):
-            at = pl.multiple_of((b * height + h) * wide, 16)
-            fp[pl.ds(at, wide), :] = jnp.zeros((wide, channels), BF16)
-            fp[pl.ds(at, width), :] = f_ref[b, h]
         at = pl.multiple_of(b * image_rows, 16)
         for c in range(3):
             shifted = gpad[:, 2 - c : 2 - c + wide, :].astype(BF16)
@@ -513,6 +517,16 @@
                 cols[pl.ds(at, image_rows), first : first + outputs] = shifted[
                     2 - a : 2 - a + height
                 ].reshape(image_rows, outputs)
+
+    f_copy.wait()
+    k_copy.start()
+
+    @pl.loop(0, images)
+    def _(b):
+        for h in range(height):
+            at = pl.multiple_of((b * height + h) * wide, 16)
+            fp[pl.ds(at, wide), :] = jnp.zeros((wide, channels), BF16)
+            fp[pl.ds(at, width), :] = f_ref[b, h]
 
     @pl.loop(0, blocks)
     def _(k):
@@ -562,8 +576,7 @@
         send(("swap", t), parts.at[t, 1 - core], swap.at[t], partner)
 
     def add(dst, src, dst_first, count, src_first=0):
-        @pl.loop(0, count)
-        def _(i):
+        for i in range(count):
             dst[dst_first + i] = dst[dst_first + i] + src[src_first + i]
 
     def mine(t, half):
@@ -575,7 +588,12 @@
     def swapped(t):
         arrive(("swap", t))
         for half in range(2):
-            add(mine(t, half), swap.at[t, half], 0, groups)
+            dst, src = mine(t, half), swap.at[t, half]
+
+            @pl.loop(0, groups, step=8)
+            def _(i):
+                for j in range(8):
+                    dst[i + j] = dst[i + j] + src[i + j]
 
     def plane1(t):
         for half in range(2):
@@ -901,6 +919,12 @@
             )
             o_ref[b, :, :, at] = out.astype(BF16).reshape(height, wide, LANES)[:, :width]
 
+    puts = []
+
+    def put(b):
+        puts.append(pltpu.make_async_copy(o_ref.at[b], o_hbm.at[b], o_sem.at[b]))
+        puts[-1].start()
+
     def whitened(t):
         both = known[0, packed : packed + 1] / pixel_total
         mean = jnp.broadcast_to(both, (LANES, LANES)).T[:group]
@@ -922,6 +946,10 @@
         arrive(("m", t))
         there = pl.ds(pl.multiple_of((1 - core) * LANES, LANES), LANES)
         share_ref[t, :, there] = mixed_in[t]
+        puts.append(
+            pltpu.make_async_copy(share_ref.at[t], share_hbm.at[t], o_sem.at[images + t])
+        )
+        puts[-1].start()
 
     p = first_plane
     e = first_depth
@@ -957,6 +985,8 @@
     plane2(p[0])
     swapped(p[4])
     k_copy.wait()
+    v_copy.wait()
+    val_copy.wait()
     back_part(0, 0)
     back_part(0, 1)
     early2_start(e[0], 0)
@@ -1032,10 +1062,13 @@
     depth2(p[6])
     whitened(p[4])
     final_part(1)
+    put(1)
     final_part(3)
+    put(3)
     depth3(p[5])
     whitened(p[5])
     final_part(5)
+    put(5)
     whitened(p[1])
     whitened(e[1])
     whitened(e[0])
@@ -1043,6 +1076,7 @@
     whitened(p[0])
     finished(p[5])
     final_part(0)
+    put(0)
     whitened(p[3])
     finished(p[1])
     depth3(p[6])
@@ -1050,11 +1084,34 @@
     finished(e[0])
     finished(e[1])
     final_part(4)
+    put(4)
     finished(p[0])
     final_part(2)
+    put(2)
     finished(p[3])
     finished(p[4])
     finished(p[6])
+    for move in puts:
+        move.wait()
+
+
+def place_kernel(held, share, placed, given, page, sheet, sems):
+    count = held.shape[0]
+    pairs = [(share, sheet, given)]
+    pairs += [(held.at[b], page.at[b], placed.at[b]) for b in range(count)]
+    loads = [
+        pltpu.make_async_copy(src, mid, sems.at[0, i]) for i, (src, mid, _) in enumerate(pairs)
+    ]
+    stores = [
+        pltpu.make_async_copy(mid, dst, sems.at[1, i]) for i, (_, mid, dst) in enumerate(pairs)
+    ]
+    for load in loads:
+        load.start()
+    for load, store in zip(loads, stores):
+        load.wait()
+        store.start()
+    for store in stores:
+        store.wait()
 
 
 def plan_local(shape, features, grads, kernel, vectors, values):
@@ -1072,7 +1129,7 @@
     quarter = group // 2
     stat_rows = quarter // 2 + 8
     sizes = (images, height, width, wide, channels, outputs, group, depth, pixel_total)
-    vmem = pl.BlockSpec(memory_space=pltpu.VMEM)
+    anywhere = pl.BlockSpec(memory_space=pl.ANY)
     sem_count = 192
     f32 = [
         (9, PAIR, 2, groups, quarter, LANES),
@@ -1095,15 +1152,21 @@
         (PAIR, stat_rows, LANES),
         (PAIR, groups, stat_rows, LANES),
     ]
-    input_grad, share = pl.pallas_call(
+    held, share = pl.pallas_call(
         functools.partial(plan_kernel, sizes),
         out_shape=(
             jax.ShapeDtypeStruct(features.shape, BF16),
             jax.ShapeDtypeStruct((9, channels // devices, outputs), F32),
         ),
-        in_specs=[vmem, vmem, pl.BlockSpec(memory_space=pl.ANY), vmem, vmem],
-        out_specs=(vmem, vmem),
+        in_specs=[anywhere] * 5,
+        out_specs=(anywhere, anywhere),
         scratch_shapes=[
+            pltpu.VMEM(features.shape, BF16),
+            pltpu.VMEM(grads.shape, BF16),
+            pltpu.VMEM(vectors.shape, F32),
+            pltpu.VMEM(values.shape, F32),
+            pltpu.VMEM(features.shape, BF16),
+            pltpu.VMEM((9, channels // devices, outputs), F32),
             pltpu.VMEM((kp, channels), BF16),
             pltpu.VMEM((channels + 16, kp), BF16),
             pltpu.VMEM((kp, 3 * taps), BF16),
@@ -1118,6 +1181,8 @@
         + [pltpu.VMEM(s, F32) for s in f32]
         + [
             pltpu.SemaphoreType.DMA,
+            pltpu.SemaphoreType.DMA((4,)),
+            pltpu.SemaphoreType.DMA((images + 9,)),
             pltpu.SemaphoreType.DMA((sem_count,)),
             pltpu.SemaphoreType.DMA((sem_count,)),
             pltpu.SemaphoreType.REGULAR((4,)),
@@ -1128,6 +1193,22 @@
         name="step",
     )(features, grads, kernel.reshape(3 * taps, channels), vectors, values)
     per = channels // devices
+    input_grad, share = pl.pallas_call(
+        place_kernel,
+        out_shape=(
+            jax.ShapeDtypeStruct(features.shape, BF16),
+            jax.ShapeDtypeStruct((9, per, outputs), F32),
+        ),
+        in_specs=[anywhere, anywhere],
+        out_specs=(anywhere, anywhere),
+        scratch_shapes=[
+            pltpu.VMEM(features.shape, BF16),
+            pltpu.VMEM((9, per, outputs), F32),
+            pltpu.SemaphoreType.DMA((2, images + 1)),
+        ],
+        compiler_params=pltpu.CompilerParams(vmem_limit_bytes=VMEM_LIMIT),
+        name="place",
+    )(held, share)
     return (input_grad, share.reshape(3, 3, per, outputs).transpose(2, 0, 1, 3))
 
 

time: 71.2 us -> 67.7 us (0.951)
  local copies, waits for them, and re-layouts: 4.55 us -> 0 us
  Pallas kernels: 65.9 us -> 66.8 us
    unnamed x4 -> x0, local copies, waits for them, and re-layouts: 4.55 us -> none
    pallas_call x0 -> x1, Pallas kernels: none -> 2.75 us  [plan_local(): pl.pallas_call(place_kernel, out_shape=(jax.ShapeDtypeStruct(features.sha...]
    pallas_call x1, Pallas kernels: 65.9 us -> 64 us  [plan_local(): pl.pallas_call(functools.partial(plan_kernel, sizes), out_shape=(jax.Shap...]
where the time goes in v3:
time: 67.7 us; the launch traced here: 67.6 us
  Pallas kernels  66.8 us (99%)
  between operations  0.8 us (1%)
    pallas_call x1, Pallas kernels, plan_local(): pl.pallas_call(functools.partial(plan_kernel, sizes), out_shape=(jax.Shap...  64 us
    pallas_call x1, Pallas kernels, plan_local(): pl.pallas_call(place_kernel, out_shape=(jax.ShapeDtypeStruct(features.sha...  2.75 us

profile of v3, /device:TPU:0, one launch (start us, length us, event | category | flops | bytes accessed | tf_op | source)
XLA Modules:
  0.0 67.6 jit_solution(11259599397821633600)
XLA Ops:
  0.6 64.0 %step.1 = (bf16[6,14,14,1024]{3,2,1,0:T(8,128)(2,1)}, f32[9,32,256]{2,1,0:T(8,128)}) custom-call(bf16[6,14,14,1024]{3,2,1,0:T(8,128)(2,1)} %f_hbm.1, bf16[6,14,14,256]{3,2,1,0:T(8,128)(2,1)} %g_hbm.1, bf16[2304,1024]{1,0:T(8,128)(2,1)} %bitcast.4, f32[16,64,64]{2,1,0:T(8,128)} %v_hbm.1, f32[16,64]{1,0:T(8,128)} %val_hbm.1), custom_call_target="tpu_custom_call" | custom-call | tf_op jit(solution)/shard_map/step/pallas_call | solution.py:1155
  64.6 2.8 %place.1 = (bf16[6,14,14,1024]{3,2,1,0:T(8,128)(2,1)}, f32[9,32,256]{2,1,0:T(8,128)}) custom-call(bf16[6,14,14,1024]{3,2,1,0:T(8,128)(2,1)} %get-tuple-element.6.held, f32[9,32,256]{2,1,0:T(8,128)} %get-tuple-element.7.share), custom_call_target="tpu_custom_call" | custom-call | tf_op jit(solution)/shard_map/place/pallas_call | solution.py:1196

commit v4 on v3

--- a/solution.py
+++ b/solution.py
@@ -961,16 +961,16 @@
     spread(2)
     tile(p[1])
     spread(3)
+    swapped(p[0])
+    plane1(p[0])
     tile(e[1])
     spread_done()
-    swapped(p[0])
-    plane1(p[0])
+    swapped(e[0])
+    early1_start(e[0], 0)
+    early1_start(e[0], 1)
     tile(p[2])
-    swapped(e[0])
     swapped(p[1])
     plane1(p[1])
-    early1_start(e[0], 0)
-    early1_start(e[0], 1)
     tile(p[3])
     swapped(e[1])
     early1_start(e[1], 0)
@@ -1058,38 +1058,38 @@
     depth3(p[4])
     depth3(p[1])
     stat6()
-    whitened(p[2])
     depth2(p[6])
-    whitened(p[4])
+    final_part(0)
+    put(0)
     final_part(1)
     put(1)
+    final_part(2)
+    put(2)
     final_part(3)
     put(3)
-    depth3(p[5])
-    whitened(p[5])
+    final_part(4)
+    put(4)
     final_part(5)
     put(5)
+    depth3(p[5])
+    whitened(e[0])
+    whitened(e[1])
+    whitened(p[0])
     whitened(p[1])
-    whitened(e[1])
-    whitened(e[0])
-    finished(p[2])
-    whitened(p[0])
-    finished(p[5])
-    final_part(0)
-    put(0)
+    whitened(p[2])
     whitened(p[3])
-    finished(p[1])
+    whitened(p[4])
+    whitened(p[5])
     depth3(p[6])
     whitened(p[6])
     finished(e[0])
     finished(e[1])
-    final_part(4)
-    put(4)
     finished(p[0])
-    final_part(2)
-    put(2)
+    finished(p[1])
+    finished(p[2])
     finished(p[3])
     finished(p[4])
+    finished(p[5])
     finished(p[6])
     for move in puts:
         move.wait()

time: 67.7 us -> 66.6 us (0.984)
  Pallas kernels: 66.8 us -> 65.6 us
    pallas_call x1, Pallas kernels: 64 us -> 62.9 us  [plan_local(): pl.pallas_call(functools.partial(plan_kernel, sizes), out_shape=(jax.Shap...]
where the time goes in v4:
time: 66.6 us; the launch traced here: 66.4 us
  Pallas kernels  65.6 us (98%)
  between operations  0.8 us (1%)
    pallas_call x1, Pallas kernels, plan_local(): pl.pallas_call(functools.partial(plan_kernel, sizes), out_shape=(jax.Shap...  62.9 us
    pallas_call x1, Pallas kernels, plan_local(): pl.pallas_call(place_kernel, out_shape=(jax.ShapeDtypeStruct(features.sha...  2.75 us

profile of v4, /device:TPU:0, one launch (start us, length us, event | category | flops | bytes accessed | tf_op | source)
XLA Modules:
  0.0 66.4 jit_solution(5632971237929605599)
XLA Ops:
  0.6 62.9 %step.1 = (bf16[6,14,14,1024]{3,2,1,0:T(8,128)(2,1)}, f32[9,32,256]{2,1,0:T(8,128)}) custom-call(bf16[6,14,14,1024]{3,2,1,0:T(8,128)(2,1)} %f_hbm.1, bf16[6,14,14,256]{3,2,1,0:T(8,128)(2,1)} %g_hbm.1, bf16[2304,1024]{1,0:T(8,128)(2,1)} %bitcast.4, f32[16,64,64]{2,1,0:T(8,128)} %v_hbm.1, f32[16,64]{1,0:T(8,128)} %val_hbm.1), custom_call_target="tpu_custom_call" | custom-call | tf_op jit(solution)/shard_map/step/pallas_call | solution.py:1155
  63.5 2.8 %place.1 = (bf16[6,14,14,1024]{3,2,1,0:T(8,128)(2,1)}, f32[9,32,256]{2,1,0:T(8,128)}) custom-call(bf16[6,14,14,1024]{3,2,1,0:T(8,128)(2,1)} %get-tuple-element.6.held, f32[9,32,256]{2,1,0:T(8,128)} %get-tuple-element.7.share), custom_call_target="tpu_custom_call" | custom-call | tf_op jit(solution)/shard_map/place/pallas_call | solution.py:1196
